TPU v7x, 32 devices: a whole 2x2x4 slice. The times are simulated.
32 devices in a mesh: rep: 2 (over x), px: 4 (over y, core), py: 4 (over z).
Axes of the slice: x: 2, y: 2, z: 4, core: 2. Of those that a mesh axis runs over, the one named last changes fastest.
Arguments:
- density: float32 [4, 128, 128, 128], P('rep', 'px', 'py'), parts along dimension 0, may hold values from -6 to 6
- kernel_factors: float32 [3, 89, 256], replicated, as said below
Outputs:
- potential: float32 [4, 128, 128, 128], P('rep', 'px', 'py'), parts along dimension 0
There are 2 independent parts, one for each index of `rep`. A program takes and returns all parts, laid end to end along the dimension named above; an argument that names none is the same for every part. Nothing has to cross between parts.
Inputs may be any that keep to these rules, and one draw needn't show every extreme that they name: Each factor is even in its frequency, kernel_factors[d, g, k] = kernel_factors[d, g, 256 - k], and is zero at k = 128.
All inputs are finite; a program needn't handle non-finite values.
Results may differ from a plain program's by a relative error of at most 0.00005.
Values sent between devices are 32-bit elements; how exact they have to be, the bound alone decides.
A program may use at most 128 MiB of HBM per device.

v0:
```python
import math
import jax
import jax.numpy as jnp
import numpy as np
from jax import lax
from jax.sharding import PartitionSpec as P

HIGH = lax.Precision.HIGH


def spectral_table(length, chunks):
    freq = np.arange(length).reshape(chunks, 1, length // chunks, 1)
    angle = freq * np.arange(length) % (2 * length) * (math.pi / length)
    both = np.concatenate([np.cos(angle), np.sin(angle)], 1)
    return both.reshape(2 * length, length).astype(np.float32)


def dot(spec, left, right):
    return jnp.einsum(spec, left, right, precision=HIGH, preferred_element_type=jnp.float32)


def kernel_block(factors, y_start, y_count, z_start, z_count):
    length = factors.shape[2] // 2
    weights = np.full((length,), 1.0 / length, np.float32)
    weights[0] = 0.5 / length
    factors = factors[:, :, :length] * weights
    factor_y = lax.dynamic_slice_in_dim(factors[1], y_start, y_count, 1)
    factor_z = lax.dynamic_slice_in_dim(factors[2], z_start, z_count, 1)
    pair = factor_z[:, :, None] * factor_y[:, None, :]
    return jnp.einsum("gzy,gx->zyx", pair, factors[0], precision=lax.Precision.HIGHEST)


def body(density, kernel_factors):
    replicas, rows_x, rows_y, length = density.shape
    count_px = lax.axis_size("px")
    count_py = lax.axis_size("py")
    half = count_px // replicas
    trade = [[i + half * r for r in range(replicas)] for i in range(half)]
    lines = [[r * half + i for i in range(half)] for r in range(replicas)]
    index_x = lax.axis_index("px") % half
    index_y = lax.axis_index("py")
    table_z = spectral_table(length, count_py)
    table_y = spectral_table(length, half)
    order = np.arange(length).reshape(replicas, half, rows_x).transpose(1, 0, 2).reshape(-1)
    table_x = spectral_table(length, 1)[:, order]
    held = lax.all_to_all(density, "px", 0, 0, axis_index_groups=trade, tiled=True)
    held = held.reshape(replicas * rows_x, rows_y, length)
    held = dot("kz,xyz->kyx", table_z, held)
    held = lax.all_to_all(held, "py", 0, 1, tiled=True)
    held = dot("qy,kyx->kqx", table_y, held)
    held = lax.all_to_all(held, "px", 1, 2, axis_index_groups=lines, tiled=True)
    z_freq, y_freq = (length // count_py, length // half)
    kernel = kernel_block(kernel_factors, index_x * y_freq, y_freq, index_y * z_freq, z_freq)
    held = dot("kqx,px->kqp", held, table_x)
    held = held.reshape(2, z_freq, 2, y_freq, 2, length) * kernel[None, :, None, :, None, :]
    held = held.reshape(2 * z_freq, 2 * y_freq, 2 * length)
    held = dot("kqp,px->kqx", held, table_x)
    held = lax.all_to_all(held, "px", 2, 1, axis_index_groups=lines, tiled=True)
    held = dot("kqx,qy->kyx", held, table_y)
    held = lax.all_to_all(held, "py", 1, 0, tiled=True)
    held = dot("kyx,kz->xyz", held, table_z)
    held = held.reshape(replicas, rows_x, rows_y, length)
    return lax.all_to_all(held, "px", 0, 0, axis_index_groups=trade, tiled=True)


def solution(mesh):
    placed = (P("rep", "px", "py", None), P())
    return jax.shard_map(
        body, mesh=mesh, in_specs=placed, out_specs=P("rep", "px", "py", None), check_vma=False
    )
```

profile of v0, /device:TPU:0, one launch (start us, length us, event | category | flops | bytes accessed | tf_op | source)
XLA Modules:
  0.0 359.6 jit_solution(2208279922184418932)
XLA Ops:
  0.0 18.8 %all_to_all.79 = f32[2,32,32,128]{3,2,1,0:T(8,128)S(1)} all-to-all(f32[2,32,32,128]{3,2,1,0:T(8,128)} %param.9), channel_id=1, replica_groups={{0,8},{4,12},{1,9},{5,13},{2,10},{6,14},{3,11},{7,15},{16,24},{20,28},{..., dimensions={0} | all-to-all | bytes 2097152 | tf_op jit(solution)/shard_map/all_to_all | solution.py:46
  20.4 4.5 %copy.27 = f32[256,32,64]{2,1,0:T(8,128)} copy(f32[256,32,64]{0,2,1:T(8,128)S(1)} %convolution_bitcast_fusion.2) | data formatting | bytes 4194304 | tf_op jit(solution)/shard_map/kz,xyz->kyx/transpose | solution.py:19
  24.9 5.5 %reshape.41 = f32[4,1,131072]{2,1,0:T(1,128)} reshape(f32[256,32,64]{2,1,0:T(8,128)} %copy.27) | data formatting | bytes 4194304
  30.4 5.3 %all-to-all-start.1 = ((f32[4,1,131072]{2,1,0:T(1,128)}), f32[4,1,131072]{2,1,0:T(1,128)S(1)}, u32[]{:S(2)}, u32[]{:S(2)}) async-start(f32[4,1,131072]{2,1,0:T(1,128)} %reshape.41), calls=%async_computation.1 | async-start | bytes 4194304 | tf_op jit(solution)/shard_map/all_to_all | solution.py:49
  37.1 45.8 %all-to-all-done.1 = f32[4,1,131072]{2,1,0:T(1,128)S(1)} async-done(((f32[4,1,131072]{2,1,0:T(1,128)}), f32[4,1,131072]{2,1,0:T(1,128)S(1)}, u32[]{:S(2)}, u32[]{:S(2)}) %all-to-all-start.1) | async-done | bytes 2097184 | tf_op jit(solution)/shard_map/all_to_all | solution.py:49
  84.7 7.7 %reduce = f32[4,131072]{1,0:T(4,128)S(1)} reduce(f32[4,1,131072]{2,1,0:T(1,128)} %copy-done, f32[]{:T(128)} %broadcast.3), dimensions={1}, to_apply=%all_to_all.57.reduce_sub_computation | reduce | bytes 4194308 | tf_op jit(solution)/shard_map/all_to_all | solution.py:49
  92.4 3.9 %reshape.42 = f32[256,32,64]{2,1,0:T(8,128)} reshape(f32[4,131072]{1,0:T(4,128)S(1)} %reduce) | data formatting | bytes 4194304
  99.2 5.9 %convolution_bitcast_fusion = f32[64,256,64]{1,2,0:T(8,128)} fusion(f32[64,128,64]{2,1,0:T(8,128)S(1)} %bitcast.56, f32[256,128,1]{1,0,2:T(8,128)S(1)} %copy-done.3), kind=kOutput, calls=%fused_computation.6 | convolution fusion | flops 805306368 | bytes 6422528 | tf_op jit(solution)/shard_map/qy,kyx->kqx/dot_general | solution.py:19
  105.1 9.2 %copy.30 = f32[64,256,64]{2,0,1:T(8,128)} copy(f32[64,256,64]{1,2,0:T(8,128)} %convolution_bitcast_fusion) | data formatting | bytes 8388608 | tf_op jit(solution)/shard_map/qy,kyx->kqx/transpose | solution.py:19
  114.3 8.7 %reshape.43 = f32[2,1,524288]{2,1,0:T(1,128)} reshape(f32[256,64,64]{2,1,0:T(8,128)} %bitcast.52) | data formatting | bytes 8388608
  123.0 11.9 %all_to_all.80 = f32[2,1,524288]{2,1,0:T(1,128)} all-to-all(f32[2,1,524288]{2,1,0:T(1,128)} %reshape.43), channel_id=1, replica_groups={{0,4},{8,12},{1,5},{9,13},{2,6},{10,14},{3,7},{11,15},{16,20},{24,28},{..., dimensions={0} | all-to-all | bytes 8388608 | tf_op jit(solution)/shard_map/all_to_all | solution.py:51
  134.8 16.5 %reduce.1 = f32[2,524288]{1,0:T(2,128)} reduce(f32[2,1,524288]{2,1,0:T(1,128)} %all_to_all.80, f32[]{:T(128)} %broadcast.3), dimensions={1}, to_apply=%all_to_all.61.reduce_sub_computation | reduce | bytes 8388612 | tf_op jit(solution)/shard_map/all_to_all | solution.py:51
  151.3 9.9 %reshape.44 = f32[256,64,64]{2,1,0:T(8,128)} reshape(f32[2,524288]{1,0:T(2,128)} %reduce.1) | data formatting | bytes 8388608
  161.3 15.3 %copy.49 = f32[64,2,128,64]{3,1,2,0:T(2,128)} copy(f32[64,2,128,64]{3,0,2,1:T(8,128)} %bitcast.53) | data formatting | bytes 8388608 | tf_op jit(solution)/shard_map/all_to_all | solution.py:51
  176.6 9.0 %reshape.34 = f32[2,32,2,64,128,1]{4,3,2,1,0,5:T(8,128)} reshape(f32[64,128,2,64]{3,2,1,0:T(2,128)} %bitcast.54) | data formatting | bytes 8388608 | tf_op jit(solution)/shard_map/kqx,px->kqp/dot_general | solution.py:19
  185.6 5.6 %broadcast_multiply_fusion = f32[2,32,2,64,2,128]{5,3,4,2,1,0:T(8,128)S(1)} fusion(f32[32,64,128]{2,1,0:T(8,128)S(1)} %fusion.6, f32[2,128,128,1,1,1]{2,1,0,5,4,3:T(8,128)S(1)} %copy-done.2, f32[2,32,2,64,128,1]{4,3,2,1,0,5:T(8,128)} %reshape.34), kind=kOutput, calls=%fused_computation.5 | convolution fusion | flops 1612709888 | bytes 13762560 | tf_op jit(solution)/shard_map/kqx,px->kqp/dot_general | solution.py:19
  191.1 7.7 %copy.34 = f32[2,32,2,64,2,128]{5,4,3,2,1,0:T(2,128)} copy(f32[2,32,2,64,2,128]{5,3,4,2,1,0:T(8,128)S(1)} %broadcast_multiply_fusion) | data formatting | bytes 16777216 | tf_op jit(solution)/shard_map/mul | solution.py:55
  198.9 11.5 %reshape.22 = f32[64,128,256]{2,1,0:T(8,128)} reshape(f32[2,32,2,64,2,128]{5,4,3,2,1,0:T(2,128)} %copy.34) | data formatting | bytes 16777216 | tf_op jit(solution)/shard_map/reshape | solution.py:56
  210.4 8.8 %fusion.11 = f32[64,128,128]{2,1,0:T(8,128)} fusion(f32[64,128,256]{2,1,0:T(8,128)} %reshape.22, f32[256,128,1]{1,0,2:T(8,128)S(1)} %copy-done.1), kind=kOutput, calls=%fused_computation.18 | convolution fusion | flops 1610612736 | bytes 12713984 | tf_op jit(solution)/shard_map/kqp,px->kqx/dot_general | solution.py:19
  219.2 5.4 %copy.35 = f32[64,128,128]{1,0,2:T(8,128)} copy(f32[64,128,128]{2,1,0:T(8,128)} %fusion.11) | data formatting | bytes 8388608 | tf_op jit(solution)/shard_map/kqp,px->kqx/dot_general | solution.py:19
  224.6 12.1 %all_to_all.81 = f32[64,128,128]{1,0,2:T(8,128)} all-to-all(f32[64,128,128]{1,0,2:T(8,128)} %copy.35), channel_id=1, replica_groups={{0,4},{8,12},{1,5},{9,13},{2,6},{10,14},{3,7},{11,15},{16,20},{24,28},{..., dimensions={2} | all-to-all | bytes 8388608 | tf_op jit(solution)/shard_map/all_to_all | solution.py:58
  236.7 5.4 %copy.36 = f32[64,128,128]{2,1,0:T(8,128)} copy(f32[64,128,128]{1,0,2:T(8,128)} %all_to_all.81) | data formatting | bytes 8388608 | tf_op jit(solution)/shard_map/all_to_all | solution.py:58
  242.1 7.0 %reshape.24 = f32[64,256,64]{2,1,0:T(8,128)} reshape(f32[64,128,128]{2,1,0:T(8,128)} %copy.36) | data formatting | bytes 8388608 | tf_op jit(solution)/shard_map/kqx,qy->kyx/dot_general | solution.py:19
  249.1 10.0 %convolution_bitcast_fusion.1 = f32[64,128,64]{1,2,0:T(8,128)S(1)} fusion(f32[64,256,64]{2,1,0:T(8,128)} %reshape.24, f32[256,128,1]{1,0,2:T(8,128)S(1)} %copy-done.6), kind=kOutput, calls=%fused_computation.7 | convolution fusion | flops 805306368 | bytes 6422528 | tf_op jit(solution)/shard_map/kqx,qy->kyx/dot_general | solution.py:19
  259.1 4.5 %copy.38 = f32[64,128,64]{2,0,1:T(8,128)} copy(f32[64,128,64]{1,2,0:T(8,128)S(1)} %convolution_bitcast_fusion.1) | data formatting | bytes 4194304 | tf_op jit(solution)/shard_map/kqx,qy->kyx/transpose | solution.py:19
  263.6 4.5 %reshape.45 = f32[4,1,131072]{2,1,0:T(1,128)S(1)} reshape(f32[128,64,64]{2,1,0:T(8,128)} %bitcast.55) | data formatting | bytes 4194304
  268.1 52.0 %all_to_all.82 = f32[4,1,131072]{2,1,0:T(1,128)} all-to-all(f32[4,1,131072]{2,1,0:T(1,128)S(1)} %reshape.45), channel_id=1, replica_groups=mesh['rep'=2,'px'=4,'py'=4] {'py'}, dimensions={0} | all-to-all | bytes 4194304 | tf_op jit(solution)/shard_map/all_to_all | solution.py:60
  320.1 7.7 %reduce.2 = f32[4,131072]{1,0:T(4,128)S(1)} reduce(f32[4,1,131072]{2,1,0:T(1,128)} %all_to_all.82, f32[]{:T(128)} %broadcast.3), dimensions={1}, to_apply=%all_to_all.68.reduce_sub_computation | reduce | bytes 4194308 | tf_op jit(solution)/shard_map/all_to_all | solution.py:60
  327.9 3.9 %reshape.46 = f32[128,64,64]{2,1,0:T(8,128)} reshape(f32[4,131072]{1,0:T(4,128)S(1)} %reduce.2) | data formatting | bytes 4194304
  331.8 4.7 %copy.39 = f32[64,128,64]{2,1,0:T(8,128)S(1)} copy(f32[64,128,64]{2,0,1:T(8,128)} %bitcast.59) | data formatting | bytes 4194304 | tf_op jit(solution)/shard_map/all_to_all | solution.py:60
  336.5 5.2 %fusion.2 = f32[32,64,128]{2,1,0:T(8,128)S(1)} fusion(f32[256,128,1]{1,0,2:T(8,128)S(1)} %copy-done.5, f32[256,32,64]{2,1,0:T(8,128)S(1)} %bitcast.57), kind=kOutput, calls=%fused_computation.3 | convolution fusion | flops 402653184 | bytes 3276800 | tf_op jit(solution)/shard_map/kyx,kz->xyz/dot_general | solution.py:19
  342.3 15.8 %all_to_all.83 = f32[2,32,32,128]{3,2,1,0:T(8,128)S(1)} all-to-all(f32[2,32,32,128]{3,2,1,0:T(8,128)S(1)} %copy.41), channel_id=1, replica_groups={{0,8},{4,12},{1,9},{5,13},{2,10},{6,14},{3,11},{7,15},{16,24},{20,28},{..., dimensions={0} | all-to-all | bytes 2097152 | tf_op jit(solution)/shard_map/all_to_all | solution.py:63
  (31 shorter events, 9.2 us)
Async XLA Ops:
  0.0 19.4 %copy-start.4 = (f32[256,128,1]{1,0,2:T(8,128)S(1)}, f32[256,128,1]{1,0,2:T(8,128)}, u32[]{:S(2)}) copy-start(f32[256,128,1]{1,0,2:T(8,128)} %constant.48) | copy-start | bytes 393220
  24.9 10.8 %copy-start.7 = (f32[3,89,256]{2,1,0:T(8,128)S(1)}, f32[3,89,256]{2,1,0:T(8,128)}, u32[]{:S(2)}) copy-start(f32[3,89,256]{2,1,0:T(8,128)} %param.10) | copy-start | bytes 820228
  24.9 10.8 %copy-start.8 = (f32[128]{0:T(128)S(1)}, f32[128]{0:T(128)}, u32[]{:S(2)}) copy-start(f32[128]{0:T(128)} %constant.39.clone) | copy-start | bytes 1540
  30.4 52.4 %all-to-all-start.1 = ((f32[4,1,131072]{2,1,0:T(1,128)}), f32[4,1,131072]{2,1,0:T(1,128)S(1)}, u32[]{:S(2)}, u32[]{:S(2)}) async-start(f32[4,1,131072]{2,1,0:T(1,128)} %reshape.41), calls=%async_computation.1 | async-start | bytes 4194304 | tf_op jit(solution)/shard_map/all_to_all | solution.py:49
  82.9 1.3 copy-start
  96.4 2.9 copy-start.3
  176.6 9.0 %copy-start.2 = (f32[2,128,128,1,1,1]{2,1,0,5,4,3:T(8,128)S(1)}, f32[2,128,128,1,1,1]{2,1,0,5,4,3:T(8,128)}, u32[]{:S(2)}) copy-start(f32[2,128,128,1,1,1]{2,1,0,5,4,3:T(8,128)} %constant.50) | copy-start | bytes 393220
  198.9 11.5 %copy-start.1 = (f32[256,128,1]{1,0,2:T(8,128)S(1)}, f32[256,128,1]{1,0,2:T(8,128)}, u32[]{:S(2)}) copy-start(f32[256,128,1]{1,0,2:T(8,128)} %constant.51) | copy-start | bytes 393220
  242.1 7.0 %copy-start.6 = (f32[256,128,1]{1,0,2:T(8,128)S(1)}, f32[256,128,1]{1,0,2:T(8,128)}, u32[]{:S(2)}) copy-start(f32[256,128,1]{1,0,2:T(8,128)} %constant.52) | copy-start | bytes 393220
  331.8 4.7 %copy-start.5 = (f32[256,128,1]{1,0,2:T(8,128)S(1)}, f32[256,128,1]{1,0,2:T(8,128)}, u32[]{:S(2)}) copy-start(f32[256,128,1]{1,0,2:T(8,128)} %constant.53) | copy-start | bytes 393220
where the time goes:
time: 365 us; the launch traced here: 360 us
  local copies, waits for them, and re-layouts  128 us (35%)
  blocking collectives  111 us (30%)
  waiting for transfers between devices  45.8 us (13%)
  matrix products  37.4 us (10%)
  other arithmetic  31.9 us (9%)
  starting transfers between devices  5.28 us (1%)
    all_to_all x1, blocking collectives, body(): held = lax.all_to_all(held, 'py', 1, 0, tiled=True)  52 us
    all_to_all x1, waiting for transfers between devices, body(): held = lax.all_to_all(held, 'py', 0, 1, tiled=True)  45.8 us
    unnamed x25, local copies, waits for them, and re-layouts  38.9 us
    dot_general x6, matrix products, dot(): jnp.einsum(spec, left, right, precision=HIGH, preferred_element_type=jnp....  36.5 us
    dot_general x3, local copies, waits for them, and re-layouts, dot(): jnp.einsum(spec, left, right, precision=HIGH, preferred_element_type=jnp....  21.4 us
    all_to_all x1, blocking collectives, body(): lax.all_to_all(density, 'px', 0, 0, axis_index_groups=trade, tiled=True)  18.8 us
    transpose x3, local copies, waits for them, and re-layouts, dot(): jnp.einsum(spec, left, right, precision=HIGH, preferred_element_type=jnp....  18.1 us
    all_to_all x1, other arithmetic, body(): held = lax.all_to_all(held, 'px', 1, 2, axis_index_groups=lines, tiled=True)  16.5 us
  transfers between devices with their start and end apart: 1, of which 1 were waited for; matrix products, arithmetic and copies ran while one was open for 0% of the time, Pallas kernels for 0%

commit v1 on v0

--- a/solution.py
+++ b/solution.py
@@ -4,6 +4,7 @@
 import numpy as np
 from jax import lax
 from jax.sharding import PartitionSpec as P
+from jax.lax import all_to_all, axis_size
 
 HIGH = lax.Precision.HIGH
 
@@ -31,6 +32,12 @@
 
 
 def body(density, kernel_factors):
+
+    def lead_grid(arr_in):
+        return jnp.concatenate(
+            all_to_all(jnp.stack(jnp.split(arr_in, axis_size("py"), axis=0)), "py", 0, 0), axis=1
+        )
+
     replicas, rows_x, rows_y, length = density.shape
     count_px = lax.axis_size("px")
     count_py = lax.axis_size("py")
@@ -46,7 +53,7 @@
     held = lax.all_to_all(density, "px", 0, 0, axis_index_groups=trade, tiled=True)
     held = held.reshape(replicas * rows_x, rows_y, length)
     held = dot("kz,xyz->kyx", table_z, held)
-    held = lax.all_to_all(held, "py", 0, 1, tiled=True)
+    held = lead_grid(held)
     held = dot("qy,kyx->kqx", table_y, held)
     held = lax.all_to_all(held, "px", 1, 2, axis_index_groups=lines, tiled=True)
     z_freq, y_freq = (length // count_py, length // half)

time: 365 us -> 363 us (level)
    reshape x0 -> x1, local copies, waits for them, and re-layouts: none -> 4.95 us  [lead_grid(): jnp.concatenate(all_to_all(jnp.stack(jnp.split(arr_in, axis_size('py'), a...]
    transpose x3 -> x2, local copies, waits for them, and re-layouts: 18.1 us -> 13.6 us  [dot(): jnp.einsum(spec, left, right, precision=HIGH, preferred_element_type=jnp....]
where the time goes in v1:
time: 363 us; the launch traced here: 358 us
  local copies, waits for them, and re-layouts  126 us (35%)
  blocking collectives  111 us (31%)
  waiting for transfers between devices  45.9 us (13%)
  matrix products  35.3 us (10%)
  other arithmetic  34.3 us (9%)
  starting transfers between devices  5.3 us (1%)
    all_to_all x1, blocking collectives, body(): held = lax.all_to_all(held, 'py', 1, 0, tiled=True)  52 us
    all_to_all x1, waiting for transfers between devices, lead_grid(): all_to_all(jnp.stack(jnp.split(arr_in, axis_size('py'), axis=0)), 'py', 0...  45.9 us
    unnamed x25, local copies, waits for them, and re-layouts  38.9 us
    dot_general x6, matrix products, dot(): jnp.einsum(spec, left, right, precision=HIGH, preferred_element_type=jnp....  34.3 us
    dot_general x3, local copies, waits for them, and re-layouts, dot(): jnp.einsum(spec, left, right, precision=HIGH, preferred_element_type=jnp....  21.4 us
    all_to_all x1, blocking collectives, body(): lax.all_to_all(density, 'px', 0, 0, axis_index_groups=trade, tiled=True)  18.8 us
    all_to_all x1, other arithmetic, body(): held = lax.all_to_all(held, 'px', 1, 2, axis_index_groups=lines, tiled=True)  16.5 us
    all_to_all x1, blocking collectives, body(): return lax.all_to_all(held, 'px', 0, 0, axis_index_groups=trade, tiled=True)  15.8 us
  transfers between devices with their start and end apart: 1, of which 1 were waited for; matrix products, arithmetic and copies ran while one was open for 0% of the time, Pallas kernels for 0%

profile of v1, /device:TPU:0, one launch (start us, length us, event | category | flops | bytes accessed | tf_op | source)
XLA Modules:
  0.0 358.3 jit_solution(18320046844317106124)
XLA Ops:
  0.0 18.8 %all_to_all.66 = f32[2,32,32,128]{3,2,1,0:T(8,128)S(1)} all-to-all(f32[2,32,32,128]{3,2,1,0:T(8,128)} %param.9), channel_id=1, replica_groups={{0,8},{4,12},{1,9},{5,13},{2,10},{6,14},{3,11},{7,15},{16,24},{20,28},{..., dimensions={0} | all-to-all | bytes 2097152 | tf_op jit(solution)/shard_map/all_to_all | solution.py:53
  23.6 5.5 %reshape.49 = f32[4,1,131072]{2,1,0:T(1,128)} reshape(f32[4,32,64,64]{3,2,1,0:T(8,128)} %fusion.11) | data formatting | bytes 4194304
  29.2 5.3 %all-to-all-start.1 = ((f32[4,1,131072]{2,1,0:T(1,128)}), f32[4,1,131072]{2,1,0:T(1,128)S(1)}, u32[]{:S(2)}, u32[]{:S(2)}) async-start(f32[4,1,131072]{2,1,0:T(1,128)} %reshape.49), calls=%async_computation.1 | async-start | bytes 4194304 | tf_op jit(solution)/shard_map/all_to_all | solution.py:38
  35.9 45.9 %all-to-all-done.1 = f32[4,1,131072]{2,1,0:T(1,128)S(1)} async-done(((f32[4,1,131072]{2,1,0:T(1,128)}), f32[4,1,131072]{2,1,0:T(1,128)S(1)}, u32[]{:S(2)}, u32[]{:S(2)}) %all-to-all-start.1) | async-done | bytes 2097184 | tf_op jit(solution)/shard_map/all_to_all | solution.py:38
  83.6 7.7 %reduce = f32[4,131072]{1,0:T(4,128)S(1)} reduce(f32[4,1,131072]{2,1,0:T(1,128)} %copy-done, f32[]{:T(128)} %broadcast.3), dimensions={1}, to_apply=%all_to_all.47.reduce_sub_computation | reduce | bytes 4194308 | tf_op jit(solution)/shard_map/all_to_all | solution.py:38
  91.3 3.9 %reshape.50 = f32[4,32,64,64]{3,2,1,0:T(8,128)} reshape(f32[4,131072]{1,0:T(4,128)S(1)} %reduce) | data formatting | bytes 4194304
  95.3 5.0 %copy.26 = f32[64,128,64]{1,2,0:T(8,128)S(1)} copy(f32[64,128,64]{0,2,1:T(8,128)} %bitcast.65) | data formatting | bytes 4194304 | tf_op jit(solution)/shard_map/reshape | solution.py:37
  100.2 3.7 %convolution_bitcast_fusion = f32[64,256,64]{1,2,0:T(8,128)} fusion(f32[64,128,64]{1,2,0:T(8,128)S(1)} %copy.26, f32[256,128,1]{1,0,2:T(8,128)S(1)} %copy-done.3), kind=kOutput, calls=%fused_computation.7 | convolution fusion | flops 805306368 | bytes 6422528 | tf_op jit(solution)/shard_map/qy,kyx->kqx/dot_general | solution.py:20
  104.0 9.1 %copy.27 = f32[64,256,64]{2,0,1:T(8,128)} copy(f32[64,256,64]{1,2,0:T(8,128)} %convolution_bitcast_fusion) | data formatting | bytes 8388608 | tf_op jit(solution)/shard_map/qy,kyx->kqx/transpose | solution.py:20
  113.1 8.7 %reshape.51 = f32[2,1,524288]{2,1,0:T(1,128)} reshape(f32[256,64,64]{2,1,0:T(8,128)} %bitcast.62) | data formatting | bytes 8388608
  121.8 11.9 %all_to_all.67 = f32[2,1,524288]{2,1,0:T(1,128)} all-to-all(f32[2,1,524288]{2,1,0:T(1,128)} %reshape.51), channel_id=1, replica_groups={{0,4},{8,12},{1,5},{9,13},{2,6},{10,14},{3,7},{11,15},{16,20},{24,28},{..., dimensions={0} | all-to-all | bytes 8388608 | tf_op jit(solution)/shard_map/all_to_all | solution.py:58
  133.7 16.5 %reduce.1 = f32[2,524288]{1,0:T(2,128)} reduce(f32[2,1,524288]{2,1,0:T(1,128)} %all_to_all.67, f32[]{:T(128)} %broadcast.3), dimensions={1}, to_apply=%all_to_all.48.reduce_sub_computation | reduce | bytes 8388612 | tf_op jit(solution)/shard_map/all_to_all | solution.py:58
  150.1 9.9 %reshape.52 = f32[256,64,64]{2,1,0:T(8,128)} reshape(f32[2,524288]{1,0:T(2,128)} %reduce.1) | data formatting | bytes 8388608
  160.1 15.3 %copy.45 = f32[64,2,128,64]{3,1,2,0:T(2,128)} copy(f32[64,2,128,64]{3,0,2,1:T(8,128)} %bitcast.63) | data formatting | bytes 8388608 | tf_op jit(solution)/shard_map/all_to_all | solution.py:58
  175.4 9.0 %reshape.42 = f32[2,32,2,64,128,1]{4,3,2,1,0,5:T(8,128)} reshape(f32[64,128,2,64]{3,2,1,0:T(2,128)} %bitcast.64) | data formatting | bytes 8388608 | tf_op jit(solution)/shard_map/kqx,px->kqp/dot_general | solution.py:20
  184.4 5.6 %broadcast_multiply_fusion = f32[2,32,2,64,2,128]{5,3,4,2,1,0:T(8,128)S(1)} fusion(f32[32,64,128]{2,1,0:T(8,128)S(1)} %fusion.6, f32[2,128,128,1,1,1]{2,1,0,5,4,3:T(8,128)S(1)} %copy-done.2, f32[2,32,2,64,128,1]{4,3,2,1,0,5:T(8,128)} %reshape.42), kind=kOutput, calls=%fused_computation.6 | convolution fusion | flops 1612709888 | bytes 13762560 | tf_op jit(solution)/shard_map/kqx,px->kqp/dot_general | solution.py:20
  189.9 7.7 %copy.31 = f32[2,32,2,64,2,128]{5,4,3,2,1,0:T(2,128)} copy(f32[2,32,2,64,2,128]{5,3,4,2,1,0:T(8,128)S(1)} %broadcast_multiply_fusion) | data formatting | bytes 16777216 | tf_op jit(solution)/shard_map/mul | solution.py:62
  197.7 11.5 %reshape.30 = f32[64,128,256]{2,1,0:T(8,128)} reshape(f32[2,32,2,64,2,128]{5,4,3,2,1,0:T(2,128)} %copy.31) | data formatting | bytes 16777216 | tf_op jit(solution)/shard_map/reshape | solution.py:63
  209.2 8.8 %fusion.12 = f32[64,128,128]{2,1,0:T(8,128)} fusion(f32[64,128,256]{2,1,0:T(8,128)} %reshape.30, f32[256,128,1]{1,0,2:T(8,128)S(1)} %copy-done.1), kind=kOutput, calls=%fused_computation.24 | convolution fusion | flops 1610612736 | bytes 12713984 | tf_op jit(solution)/shard_map/kqp,px->kqx/dot_general | solution.py:20
  217.9 5.4 %copy.32 = f32[64,128,128]{1,0,2:T(8,128)} copy(f32[64,128,128]{2,1,0:T(8,128)} %fusion.12) | data formatting | bytes 8388608 | tf_op jit(solution)/shard_map/kqp,px->kqx/dot_general | solution.py:20
  223.4 12.0 %all_to_all.68 = f32[64,128,128]{1,0,2:T(8,128)} all-to-all(f32[64,128,128]{1,0,2:T(8,128)} %copy.32), channel_id=1, replica_groups={{0,4},{8,12},{1,5},{9,13},{2,6},{10,14},{3,7},{11,15},{16,20},{24,28},{..., dimensions={2} | all-to-all | bytes 8388608 | tf_op jit(solution)/shard_map/all_to_all | solution.py:65
  235.4 5.4 %copy.33 = f32[64,128,128]{2,1,0:T(8,128)} copy(f32[64,128,128]{1,0,2:T(8,128)} %all_to_all.68) | data formatting | bytes 8388608 | tf_op jit(solution)/shard_map/all_to_all | solution.py:65
  240.8 7.0 %reshape.32 = f32[64,256,64]{2,1,0:T(8,128)} reshape(f32[64,128,128]{2,1,0:T(8,128)} %copy.33) | data formatting | bytes 8388608 | tf_op jit(solution)/shard_map/kqx,qy->kyx/dot_general | solution.py:20
  247.8 10.0 %convolution_bitcast_fusion.1 = f32[64,128,64]{1,2,0:T(8,128)S(1)} fusion(f32[64,256,64]{2,1,0:T(8,128)} %reshape.32, f32[256,128,1]{1,0,2:T(8,128)S(1)} %copy-done.6), kind=kOutput, calls=%fused_computation.8 | convolution fusion | flops 805306368 | bytes 6422528 | tf_op jit(solution)/shard_map/kqx,qy->kyx/dot_general | solution.py:20
  257.9 4.5 %copy.35 = f32[64,128,64]{2,0,1:T(8,128)} copy(f32[64,128,64]{1,2,0:T(8,128)S(1)} %convolution_bitcast_fusion.1) | data formatting | bytes 4194304 | tf_op jit(solution)/shard_map/kqx,qy->kyx/transpose | solution.py:20
  262.3 4.5 %reshape.53 = f32[4,1,131072]{2,1,0:T(1,128)S(1)} reshape(f32[128,64,64]{2,1,0:T(8,128)} %bitcast.66) | data formatting | bytes 4194304
  266.9 52.0 %all_to_all.69 = f32[4,1,131072]{2,1,0:T(1,128)} all-to-all(f32[4,1,131072]{2,1,0:T(1,128)S(1)} %reshape.53), channel_id=1, replica_groups=mesh['rep'=2,'px'=4,'py'=4] {'py'}, dimensions={0} | all-to-all | bytes 4194304 | tf_op jit(solution)/shard_map/all_to_all | solution.py:67
  318.9 7.7 %reduce.2 = f32[4,131072]{1,0:T(4,128)S(1)} reduce(f32[4,1,131072]{2,1,0:T(1,128)} %all_to_all.69, f32[]{:T(128)} %broadcast.3), dimensions={1}, to_apply=%all_to_all.55.reduce_sub_computation | reduce | bytes 4194308 | tf_op jit(solution)/shard_map/all_to_all | solution.py:67
  326.6 3.9 %reshape.54 = f32[128,64,64]{2,1,0:T(8,128)} reshape(f32[4,131072]{1,0:T(4,128)S(1)} %reduce.2) | data formatting | bytes 4194304
  330.5 4.7 %copy.36 = f32[64,128,64]{2,1,0:T(8,128)S(1)} copy(f32[64,128,64]{2,0,1:T(8,128)} %bitcast.68) | data formatting | bytes 4194304 | tf_op jit(solution)/shard_map/all_to_all | solution.py:67
  335.2 5.2 %fusion.2 = f32[32,64,128]{2,1,0:T(8,128)S(1)} fusion(f32[256,128,1]{1,0,2:T(8,128)S(1)} %copy-done.5, f32[256,32,64]{2,1,0:T(8,128)S(1)} %bitcast.67), kind=kOutput, calls=%fused_computation.4 | convolution fusion | flops 402653184 | bytes 3276800 | tf_op jit(solution)/shard_map/kyx,kz->xyz/dot_general | solution.py:20
  341.0 15.8 %all_to_all.70 = f32[2,32,32,128]{3,2,1,0:T(8,128)S(1)} all-to-all(f32[2,32,32,128]{3,2,1,0:T(8,128)S(1)} %copy.38), channel_id=1, replica_groups={{0,8},{4,12},{1,9},{5,13},{2,10},{6,14},{3,11},{7,15},{16,24},{20,28},{..., dimensions={0} | all-to-all | bytes 2097152 | tf_op jit(solution)/shard_map/all_to_all | solution.py:70
  (32 shorter events, 9.5 us)
Async XLA Ops:
  0.0 19.4 %copy-start.4 = (f32[256,128,1]{1,0,2:T(8,128)S(1)}, f32[256,128,1]{1,0,2:T(8,128)}, u32[]{:S(2)}) copy-start(f32[256,128,1]{1,0,2:T(8,128)} %constant.48) | copy-start | bytes 393220
  23.6 10.9 %copy-start.7 = (f32[3,89,256]{2,1,0:T(8,128)S(1)}, f32[3,89,256]{2,1,0:T(8,128)}, u32[]{:S(2)}) copy-start(f32[3,89,256]{2,1,0:T(8,128)} %param.10) | copy-start | bytes 820228
  23.6 10.9 %copy-start.8 = (f32[128]{0:T(128)S(1)}, f32[128]{0:T(128)}, u32[]{:S(2)}) copy-start(f32[128]{0:T(128)} %constant.39.clone) | copy-start | bytes 1540
  29.2 52.6 %all-to-all-start.1 = ((f32[4,1,131072]{2,1,0:T(1,128)}), f32[4,1,131072]{2,1,0:T(1,128)S(1)}, u32[]{:S(2)}, u32[]{:S(2)}) async-start(f32[4,1,131072]{2,1,0:T(1,128)} %reshape.49), calls=%async_computation.1 | async-start | bytes 4194304 | tf_op jit(solution)/shard_map/all_to_all | solution.py:38
  81.8 1.3 copy-start
  95.3 5.0 %copy-start.3 = (f32[256,128,1]{1,0,2:T(8,128)S(1)}, f32[256,128,1]{1,0,2:T(8,128)}, u32[]{:S(2)}) copy-start(f32[256,128,1]{1,0,2:T(8,128)} %constant.49) | copy-start | bytes 393220
  175.4 9.0 %copy-start.2 = (f32[2,128,128,1,1,1]{2,1,0,5,4,3:T(8,128)S(1)}, f32[2,128,128,1,1,1]{2,1,0,5,4,3:T(8,128)}, u32[]{:S(2)}) copy-start(f32[2,128,128,1,1,1]{2,1,0,5,4,3:T(8,128)} %constant.50) | copy-start | bytes 393220
  197.7 11.5 %copy-start.1 = (f32[256,128,1]{1,0,2:T(8,128)S(1)}, f32[256,128,1]{1,0,2:T(8,128)}, u32[]{:S(2)}) copy-start(f32[256,128,1]{1,0,2:T(8,128)} %constant.51) | copy-start | bytes 393220
  240.8 7.0 %copy-start.6 = (f32[256,128,1]{1,0,2:T(8,128)S(1)}, f32[256,128,1]{1,0,2:T(8,128)}, u32[]{:S(2)}) copy-start(f32[256,128,1]{1,0,2:T(8,128)} %constant.52) | copy-start | bytes 393220
  330.5 4.7 %copy-start.5 = (f32[256,128,1]{1,0,2:T(8,128)S(1)}, f32[256,128,1]{1,0,2:T(8,128)}, u32[]{:S(2)}) copy-start(f32[256,128,1]{1,0,2:T(8,128)} %constant.53) | copy-start | bytes 393220
